TPU v7x, 32 devices: a whole 2x2x4 slice. The times are simulated.
32 devices in a mesh: pts: 4 (over y, x), med: 8 (over z, core).
Axes of the slice: x: 2, y: 2, z: 4, core: 2. Of those that a mesh axis runs over, the one named last changes fastest.
Arguments:
- points: float32 [65536, 1024], P(('pts', 'med')), may hold values from -6 to 6
- weights: float32 [65536], P(('pts', 'med')), may hold values from 0.2 to 6
- medoid_ids: int32 [512], replicated, may hold values from 0 to 65535, as said below
Outputs:
- cover: float32 [65536], P(('pts', 'med'))
- total: float32 [], replicated
Inputs may be any that keep to these rules, and one draw needn't show every extreme that they name: `medoid_ids`: distinct row numbers; the points of one device hold at most 24 medoids, and some device holds exactly 24 in every draw.
All inputs are finite; a program needn't handle non-finite values.
Results may differ from a plain program's by a relative error of at most 0.00005.
Values sent between devices are 32-bit elements; how exact they have to be, the bound alone decides.
A program may use at most 128 MiB of HBM per device.

v0:
```python
import jax
import jax.numpy as jnp
from jax import lax
from jax.sharding import PartitionSpec as P

MED_DEV = 16


EPS = 1e-06


def best_match(unit, block, offset):
    sims = lax.dot_general(
        unit,
        block,
        (((1,), (1,)), ((), ())),
        precision=lax.Precision.HIGHEST,
        preferred_element_type=jnp.float32,
    )
    return jnp.max(sims + offset[None, :], axis=1)


def slot_offsets(counts, global_rows, group_pts, group_med, capacity):
    group_rows = group_pts * capacity
    med_of = global_rows // group_rows
    within = global_rows % group_rows
    pts_of = within // capacity
    slot_of = within % capacity
    device_of = pts_of * group_med + med_of
    devices = jnp.arange(group_pts * group_med, dtype=jnp.int32)
    owned_count = jnp.sum(
        jnp.where(device_of[:, None] == devices[None, :], counts[None, :], 0), axis=1
    )
    return jnp.where(slot_of < owned_count, 0.0, -4.0).astype(jnp.float32)


def body(points, weights, medoid_ids):
    rows = points.shape[0]
    capacity = MED_DEV + MED_DEV // 2
    group_pts = lax.axis_size("pts")
    group_med = lax.axis_size("med")
    unit = points * lax.rsqrt(jnp.sum(points * points, axis=1, keepdims=True) + EPS)
    med_index = lax.axis_index("med")
    row_start = (lax.axis_index("pts") * group_med + med_index) * rows
    local = medoid_ids - row_start
    owned = jnp.logical_and(local >= 0, local < rows).astype(jnp.int32)
    rank = jnp.cumsum(owned) - 1
    slot_ids = jnp.arange(capacity, dtype=jnp.int32)
    select = jnp.logical_and(owned[None, :] == 1, rank[None, :] == slot_ids[:, None]).astype(
        jnp.int32
    )
    position = jnp.sum(select * local[None, :], axis=1)
    valid = jnp.sum(select, axis=1) > 0
    mine = jnp.take(unit, position, axis=0) * valid[:, None].astype(jnp.float32)
    owner_of = medoid_ids // rows
    devices = jnp.arange(group_pts * group_med, dtype=jnp.int32)
    counts = jnp.sum((owner_of[None, :] == devices[:, None]).astype(jnp.int32), axis=1)
    block = lax.all_gather(mine, "pts", axis=0, tiled=True)
    start_best = jnp.full((rows,), -8.0, jnp.float32)
    piece = lax.all_gather(block, "med", axis=0, tiled=True)
    global_rows = jnp.arange(piece.shape[0], dtype=jnp.int32)
    piece_offset = slot_offsets(counts, global_rows, group_pts, group_med, capacity)
    cover = jnp.maximum(start_best, best_match(unit, piece, piece_offset))
    both_sums = lax.psum(jnp.stack([jnp.sum(weights * cover), jnp.sum(weights)]), ("pts", "med"))
    return (cover, both_sums[0] / both_sums[1])


def solution(mesh):
    return jax.shard_map(
        body,
        mesh=mesh,
        in_specs=(P(("pts", "med"), None), P(("pts", "med")), P()),
        out_specs=(P(("pts", "med")), P()),
        check_vma=False,
    )
```

profile of v0, /device:TPU:0, one launch (start us, length us, event | category | flops | bytes accessed | tf_op | source)
XLA Modules:
  0.0 147.5 jit_solution(15723708422780872622)
XLA Ops:
  7.2 0.0 all-gather.2.cloned.1.call-start
  7.2 0.7 convert_compare_fusion
  7.9 0.3 reduce-window.9
  8.2 0.1 slice.13
  8.3 0.0 copy-start
  8.3 0.1 slice_reduce_fusion
  8.4 0.1 add_bitcast_fusion
  8.5 0.1 convert_reduce_fusion.1
  8.7 4.1 %multiply_reduce_fusion = f32[2048]{0:T(1024)S(1)} fusion(f32[2048,1024]{1,0:T(8,128)} %param.3), kind=kLoop, calls=%fused_computation.1 | loop fusion | flops 4192256 | bytes 8396800 | tf_op jit(solution)/shard_map/reduce_sum | solution.py:42
  12.9 1.2 copy-done
  14.1 0.0 copy-start.2
  14.1 3.8 %broadcast_multiply_fusion = f32[2048,1024]{1,0:T(8,128)} fusion(f32[2048,1024]{1,0:T(8,128)S(1)} %copy-done, f32[2048]{0:T(1024)S(1)} %add_rsqrt_fusion), kind=kLoop, calls=%fused_computation.3 | loop fusion | flops 2097152 | bytes 16785408 | tf_op jit(solution)/shard_map/mul | solution.py:42
  17.9 4.0 %gather_fusion = f32[24,1024]{1,0:T(8,128)S(1)} fusion(f32[2048,1024]{1,0:T(8,128)} %broadcast_multiply_fusion, s32[1024]{0:T(1024)S(1)} %pad_clamp_fusion), kind=kCustom, calls=%fused_computation | custom fusion | bytes 196704 | tf_op jit(solution)/shard_map/jit(_take)/gather | solution.py:54
  22.0 0.1 select_multiply_fusion
  22.0 11.7 %all_gather.6 = f32[96,1024]{1,0:T(8,128)} all-gather(f32[24,1024]{1,0:T(8,128)S(1)} %select_multiply_fusion), channel_id=1, replica_groups=mesh['pts'=4,'med'=8] {'pts'}, dimensions={0}, use_global_device_ids=true | all-gather | bytes 491520 | tf_op jit(solution)/shard_map/all_gather | solution.py:58
  33.7 0.0 all-gather.2.cloned.1.call-update
  33.8 0.0 copy-done.2
  33.8 0.1 convert_reduce_fusion
  33.9 0.1 select_reduce_fusion
  34.1 0.0 copy-start.1
  34.1 38.3 %all-gather.2.cloned.1.call-done = f32[768,1024]{1,0:T(8,128)} async-done(((f32[96,1024]{1,0:T(8,128)}), f32[768,1024]{1,0:T(8,128)}) %all-gather.2.cloned.1.call-update) | async-done | bytes 3145744 | tf_op jit(solution)/shard_map/all_gather | solution.py:60
  72.4 23.2 %add_reduce_fusion = f32[2048]{0:T(1024)S(1)} fusion(f32[2048,1024]{1,0:T(8,128)} %broadcast_multiply_fusion, f32[768,1024]{1,0:T(8,128)} %all-gather.2.cloned.1.call-done, f32[768]{0:T(1024)S(1)} %fusion.14), kind=kOutput, calls=%fused_computation.2 | convolution fusion | flops 19330496512 | bytes 11545600 | tf_op jit(solution)/shard_map/dot_general | solution.py:13
  95.7 0.0 copy-done.1
  95.7 1.3 multiply_reduce_fusion.1
  97.0 1.4 pad_maximum_fusion
  98.4 39.2 %psum.7 = f32[2]{0:T(128)S(1)} all-reduce(f32[2]{0:T(128)S(1)} %pad_maximum_fusion), channel_id=1, replica_groups=mesh['pts'=4,'med'=8] {'pts','med'}, use_global_device_ids=true, to_apply=%region_10.11 | all-reduce | flops 2 | bytes 16 | tf_op jit(solution)/shard_map/psum | solution.py:64
  137.5 0.6 fusion.18
  (9 shorter events, 0.1 us)
Async XLA Ops:
  7.2 65.2 %all-gather.2.cloned.1.call-start = ((), (), s32[]{:S(2)}) async-start(), calls=%async_computation | async-start | bytes 3538944 | tf_op jit(solution)/shard_map/all_gather | solution.py:60
  8.3 5.8 %copy-start = (f32[2048,1024]{1,0:T(8,128)S(1)}, f32[2048,1024]{1,0:T(8,128)}, u32[]{:S(2)}) copy-start(f32[2048,1024]{1,0:T(8,128)} %param.3) | copy-start | bytes 25165828
  14.1 19.7 %copy-start.2 = (s32[512]{0:T(512)S(1)}, s32[512]{0:T(512)}, u32[]{:S(2)}) copy-start(s32[512]{0:T(512)} %param.5) | copy-start | bytes 6148
  34.1 61.6 %copy-start.1 = (f32[2048]{0:T(1024)S(1)}, f32[2048]{0:T(1024)}, u32[]{:S(2)}) copy-start(f32[2048]{0:T(1024)} %param.4) | copy-start | bytes 24580
Sparse Core Ops, SparseCore 0:
  33.9 38.4 all-gather.1
where the time goes:
time: 148 us; the launch traced here: 147 us
  blocking collectives  50.9 us (34%)
  waiting for transfers between devices  38.4 us (26%)
  matrix products  23.2 us (16%)
  between operations  16.6 us (11%)
  other arithmetic  12.3 us (8%)
  local copies, waits for them, and re-layouts  6.06 us (4%)
    psum x1, blocking collectives, body(): lax.psum(jnp.stack([jnp.sum(weights * cover), jnp.sum(weights)]), ('pts',...  39.2 us
    all_gather x1, waiting for transfers between devices, body(): piece = lax.all_gather(block, 'med', axis=0, tiled=True)  38.3 us
    dot_general x1, matrix products, best_match(): lax.dot_general(unit, block, (((1,), (1,)), ((), ())), precision=lax.Prec...  23.2 us
    all_gather x1, blocking collectives, body(): block = lax.all_gather(mine, 'pts', axis=0, tiled=True)  11.7 us
    reduce_sum x1, other arithmetic, body(): jnp.sum(points * points, axis=1, keepdims=True) + EPS  4.15 us
    gather x1, local copies, waits for them, and re-layouts, body(): mine = jnp.take(unit, position, axis=0) * valid[:, None].astype(jnp.float32)  4.02 us
    mul x1, other arithmetic, body(): points * lax.rsqrt(jnp.sum(points * points, axis=1, keepdims=True) + EPS)  3.83 us
  transfers between devices with their start and end apart: 1, of which 1 were waited for; matrix products, arithmetic and copies ran while one was open for 0% of the time, Pallas kernels for 0%

commit v1 on v0

v1 whole, which is shorter than its diff:
```python
import functools

import jax
import jax.numpy as jnp
from jax import lax
from jax.experimental import pallas as pl
from jax.experimental.pallas import tpu as pltpu
from jax.sharding import PartitionSpec as P

MED_DEV = 16
CAPACITY = MED_DEV + MED_DEV // 2
EPS = 1e-06
CORES = 2
TILE = 256


def gather_kernel(start_ref, ids_ref, points_ref, out_ref, pos_ref, buf_ref, sem):
    rows = points_ref.shape[0]
    start = start_ref[0]
    for slot in range(CAPACITY):
        pos_ref[slot] = 0

    def scan(step, count):
        for lane in range(8):
            local = ids_ref[step * 8 + lane] - start
            owned = jnp.logical_and(local >= 0, local < rows)
            pos_ref[count] = jnp.where(owned, local, 0)
            count = count + owned.astype(jnp.int32)
        return count

    lax.fori_loop(0, ids_ref.shape[0] // 8, scan, jnp.int32(0))

    def row_copy(slot):
        return pltpu.make_async_copy(
            points_ref.at[pl.ds(pos_ref[slot], 1)], buf_ref.at[pl.ds(slot, 1)], sem.at[slot]
        )

    for slot in range(CAPACITY):
        row_copy(slot).start()
    for slot in range(CAPACITY):
        row_copy(slot).wait()
    block = buf_ref[...]
    out_ref[...] = block * lax.rsqrt(jnp.sum(block * block, axis=1, keepdims=True) + EPS)


def split(value):
    high = value.astype(jnp.bfloat16)
    return high, (value - high.astype(jnp.float32)).astype(jnp.bfloat16)


def cover_kernel(
    group_pts, group_med, mine_ref, points_ref, weights_ref, ids_ref, cover_ref, total_ref,
    recv, pbuf, phigh, plow, chigh, clow, offs, best, scale, part, tin,
    psem, msem, rsem, zsem, fsem, ssem, bsem, tsend, trecv,
):
    rows = points_ref.shape[0]
    tiles = rows // TILE
    n_z = group_med // CORES
    n_a = 2
    n_b = group_pts // n_a
    swap = n_a == n_b
    n_1, n_2 = n_b, n_a
    me_pts = lax.axis_index("pts")
    me_med = lax.axis_index("med")
    core = lax.rem(me_med, CORES)
    zed = me_med // CORES
    a, b = me_pts // n_b, lax.rem(me_pts, n_b)
    other = 1 - core

    def axes_of(which):
        if swap:
            return jnp.where(which == 0, b, a), jnp.where(which == 0, a, b)
        return b, a

    def pts_of(which, i_1, i_2):
        if swap:
            return jnp.where(which == 0, i_2 * n_b + i_1, i_1 * n_b + i_2)
        return i_2 * n_b + i_1

    i_1, i_2 = axes_of(core)
    o_1, o_2 = axes_of(other)

    def dev_z(step):
        return {"pts": me_pts, "med": lax.rem(zed + step, n_z) * CORES + core}

    def dev_1(step):
        return {"pts": pts_of(core, lax.rem(i_1 + step, n_1), i_2), "med": me_med}

    def dev_2(step):
        return {"pts": pts_of(core, i_1, lax.rem(i_2 + step, n_2)), "med": me_med}

    sibling = {"pts": me_pts, "med": zed * CORES + other}
    partners = (
        [dev_z(step) for step in range(1, n_z)]
        + [dev_1(step) for step in range(1, n_1)]
        + [dev_2(step) for step in range(1, n_2)]
        + [sibling]
    )

    def points_copy(tile):
        part_of = pl.ds(pl.multiple_of(tile * TILE, TILE), TILE)
        return pltpu.make_async_copy(points_ref.at[part_of], pbuf.at[part_of], psem.at[tile])

    own_copy = pltpu.make_async_copy(mine_ref, recv.at[core, i_2, i_1, zed], msem)
    own_copy.start()
    for tile in range(tiles):
        points_copy(tile).start()
    barrier = pltpu.get_barrier_semaphore()
    for partner in partners:
        pl.semaphore_signal(barrier, inc=1, device_id=partner, device_id_type=pl.DeviceIdType.MESH)
    pl.semaphore_wait(barrier, len(partners))

    def send(src, j_2, j_1, z, sem, partner):
        return pltpu.make_async_remote_copy(
            src_ref=src,
            dst_ref=recv.at[core, j_2, j_1, z],
            send_sem=sem,
            recv_sem=rsem.at[core, j_2, j_1, z],
            device_id=partner,
            device_id_type=pl.DeviceIdType.MESH,
        )

    def send_z(step):
        return send(mine_ref, i_2, i_1, zed, zsem.at[step], dev_z(step))

    def send_1(z, step, src=None):
        src = recv.at[core, i_2, i_1, z] if src is None else src
        return send(src, i_2, i_1, z, fsem.at[z, step], dev_1(step))

    def send_2(j_1, z, step, src=None):
        src = recv.at[core, i_2, j_1, z] if src is None else src
        return send(src, i_2, j_1, z, ssem.at[j_1, z, step], dev_2(step))

    def send_b(j_2, j_1, z, src=None):
        src = recv.at[core, j_2, j_1, z] if src is None else src
        return send(src, j_2, j_1, z, bsem.at[j_2, j_1, z], sibling)

    def arrived(which, j_2, j_1, z):
        slot = recv.at[which, j_2, j_1, z]
        pltpu.make_async_copy(slot, slot, rsem.at[which, j_2, j_1, z]).wait()

    def z_at(step):
        return lax.rem(zed + step, n_z)

    def one_at(step):
        return lax.rem(i_1 + step, n_1)

    def two_at(step):
        return lax.rem(i_2 + step, n_2)

    for step in range(1, n_1):
        send_1(zed, step, mine_ref).start()
    for step in range(1, n_2):
        send_2(i_1, zed, step, mine_ref).start()
    for step in [1, n_z - 1] + list(range(2, n_z - 1)) if n_z > 2 else range(1, n_z):
        send_z(step).start()
    send_b(i_2, i_1, zed, mine_ref).start()

    best[...] = jnp.full(best.shape, -1e30, jnp.float32)

    def prepare(tile, carry):
        points_copy(tile).wait()
        part_of = pl.ds(pl.multiple_of(tile * TILE, TILE), TILE)
        value = pbuf[part_of, :]
        high, low = split(value)
        phigh[part_of, :] = high
        plow[part_of, :] = low
        square = value * value
        lanes = square[:, :128]
        for k in range(1, square.shape[1] // 128):
            lanes = lanes + square[:, k * 128 : (k + 1) * 128]
        norm = jnp.sum(lanes.T, axis=0, keepdims=True)
        scale[:, part_of] = jnp.broadcast_to(lax.rsqrt(norm + EPS), (8, TILE))
        return carry

    lax.fori_loop(0, tiles, prepare, 0)
    own_copy.wait()

    z_order = [1, n_z - 1] + list(range(2, n_z - 1)) if n_z > 2 else list(range(1, n_z))
    for step in z_order:
        z = z_at(step)
        arrived(core, i_2, i_1, z)
        for hop in range(1, n_1):
            send_1(z, hop).start()
        for hop in range(1, n_2):
            send_2(i_1, z, hop).start()
        send_b(i_2, i_1, z).start()

    width = n_z * CAPACITY
    ids = ids_ref[...]

    def load_chunk(which, j_2, j_1, base):
        value = recv[which, j_2, j_1].reshape(width, recv.shape[-1])
        high, low = split(value)
        chigh[base : base + width, :] = high
        clow[base : base + width, :] = low
        at = lax.broadcasted_iota(jnp.int32, (width, 1), 0)
        z = at // CAPACITY
        slot = at - z * CAPACITY
        first = (pts_of(which, j_1, j_2) * group_med + z * CORES + which) * rows
        inside = jnp.logical_and(ids >= first, ids < first + rows)
        count = jnp.sum(jnp.where(inside, 1.0, 0.0), axis=1, keepdims=True)
        offs[base : base + width, :] = jnp.where(slot.astype(jnp.float32) < count, 0.0, -1e30)

    dims = (((1,), (1,)), ((), ()))

    def multiply(tile):
        part_of = pl.ds(pl.multiple_of(tile * TILE, TILE), TILE)
        dot = functools.partial(lax.dot_general, dimension_numbers=dims, preferred_element_type=jnp.float32)
        high, low = phigh[part_of, :], plow[part_of, :]
        sims = dot(clow[...], high) + dot(chigh[...], low) + dot(chigh[...], high)
        sims = sims + offs[...]
        top = jnp.max(sims.reshape(-1, 8, TILE), axis=0)
        best[:, part_of] = jnp.maximum(best[:, part_of], top)

    def event_1(e):
        hop = e // n_z + 1
        z = z_at(lax.rem(e, n_z))
        j_1 = one_at(hop)
        arrived(core, i_2, j_1, z)
        for far in range(1, n_2):
            send_2(j_1, z, far).start()
        send_b(i_2, j_1, z).start()

    def event_2(one, e):
        hop = e // n_z + 1
        z = z_at(lax.rem(e, n_z))
        j_2 = two_at(hop)
        arrived(core, j_2, one_at(one), z)
        send_b(j_2, one_at(one), z).start()

    def chunk(e_2, e_1, event, events):
        for z in range(n_z):
            if swap:
                s_2, s_1 = lax.rem(o_2 + e_2, n_2), lax.rem(o_1 + e_1, n_1)
            else:
                s_2, s_1 = two_at(e_2), one_at(e_1)
            if not (e_2 == 0 and e_1 == 0):
                pass
            arrived(other, s_2, s_1, z)
        load_chunk(core, two_at(e_2), one_at(e_1), 0)
        load_chunk(other, s_2, s_1, width)

        def step(tile, carry):
            if events:
                @pl.when(tile < events)
                def _():
                    event(tile)
            multiply(tile)
            return carry

        lax.fori_loop(0, tiles, step, 0)
        if events > tiles:
            def rest(e, carry):
                event(e)
                return carry

            lax.fori_loop(tiles, events, rest, 0)

    order = [(e_2, e_1) for e_2 in range(n_2) for e_1 in range(n_1)]
    for e_2, e_1 in order:
        if e_2 == 0 and e_1 == 0:
            chunk(0, 0, event_1, (n_1 - 1) * n_z)
        elif e_2 == 0:
            last = e_1 == n_1 - 1
            if last:
                chunk(0, e_1, functools.partial(event_2, 0), (n_2 - 1) * n_z)
            else:
                chunk(0, e_1, None, 0)
        elif e_2 == 1:
            if e_1 + 1 < n_1:
                chunk(1, e_1, functools.partial(event_2, e_1 + 1), (n_2 - 1) * n_z)
            else:
                chunk(1, e_1, None, 0)
        else:
            chunk(e_2, e_1, None, 0)

    cover = jnp.max(best[...], axis=0, keepdims=True) * scale[0:1, :]
    cover_ref[...] = cover
    weights = weights_ref[...]
    lane = lax.broadcasted_iota(jnp.int32, (8, 128), 1)
    number = jnp.sum(weights * cover, axis=1, keepdims=True)
    weight = jnp.sum(weights, axis=1, keepdims=True)
    value = jnp.where(lane == 0, number, weight)

    stages = [
        (n_z, zed, dev_z), (n_1, i_1, dev_1), (n_2, i_2, dev_2), (CORES, core, lambda step: sibling),
    ]
    copies = []
    for stage, (extent, index, partner_of) in enumerate(stages):
        if extent == 1:
            continue
        part[stage] = value
        for step in range(1, extent):
            copy = pltpu.make_async_remote_copy(
                src_ref=part.at[stage],
                dst_ref=tin.at[stage, index],
                send_sem=tsend.at[stage, step],
                recv_sem=trecv.at[stage, index],
                device_id=partner_of(step),
                device_id_type=pl.DeviceIdType.MESH,
            )
            copy.start()
            copies.append(copy)
        for step in range(1, extent):
            where = lax.rem(index + step, extent)
            slot = tin.at[stage, where]
            pltpu.make_async_copy(slot, slot, trecv.at[stage, where]).wait()
        tin[stage, index] = value
        value = tin[stage, 0]
        for at in range(1, extent):
            value = value + tin[stage, at]
    total_ref[...] = value[:, 0:1] / value[:, 1:2] + jnp.zeros((8, 128), jnp.float32)

    for step in range(1, n_z):
        send_z(step).wait_send()
    for z in range(n_z):
        for step in range(1, n_1):
            send_1(z, step).wait_send()
        for j_1 in range(n_1):
            for step in range(1, n_2):
                send_2(j_1, z, step).wait_send()
            for j_2 in range(n_2):
                send_b(j_2, j_1, z).wait_send()
    for copy in copies:
        copy.wait_send()


def body(points, weights, medoid_ids):
    rows, width = points.shape
    group_pts = lax.axis_size("pts")
    group_med = lax.axis_size("med")
    n_z, n_a = group_med // CORES, 2
    n_1, n_2 = group_pts // n_a, n_a
    start = (lax.axis_index("pts") * group_med + lax.axis_index("med")) * rows
    smem = pl.BlockSpec(memory_space=pltpu.SMEM)
    vmem = pl.BlockSpec(memory_space=pltpu.VMEM)
    hbm = pl.BlockSpec(memory_space=pl.ANY)
    mine = pl.pallas_call(
        gather_kernel,
        out_shape=jax.ShapeDtypeStruct((CAPACITY, width), jnp.float32),
        in_specs=[smem, smem, hbm],
        out_specs=vmem,
        scratch_shapes=[
            pltpu.SMEM((CAPACITY + 1,), jnp.int32),
            pltpu.VMEM((CAPACITY, width), jnp.float32),
            pltpu.SemaphoreType.DMA((CAPACITY,)),
        ],
        name="gather_rows",
    )(start[None].astype(jnp.int32), medoid_ids, points)

    chunk = CORES * n_z * CAPACITY
    top = max(n_z, n_1, n_2, CORES)
    dma = pltpu.SemaphoreType.DMA
    cover, total = pl.pallas_call(
        functools.partial(cover_kernel, group_pts, group_med),
        out_shape=[
            jax.ShapeDtypeStruct((1, rows), jnp.float32),
            jax.ShapeDtypeStruct((8, 128), jnp.float32),
        ],
        in_specs=[vmem, hbm, vmem, vmem],
        out_specs=[vmem, vmem],
        scratch_shapes=[
            pltpu.VMEM((CORES, n_2, n_1, n_z, CAPACITY, width), jnp.float32),
            pltpu.VMEM((rows, width), jnp.float32),
            pltpu.VMEM((rows, width), jnp.bfloat16),
            pltpu.VMEM((rows, width), jnp.bfloat16),
            pltpu.VMEM((chunk, width), jnp.bfloat16),
            pltpu.VMEM((chunk, width), jnp.bfloat16),
            pltpu.VMEM((chunk, 1), jnp.float32),
            pltpu.VMEM((8, rows), jnp.float32),
            pltpu.VMEM((8, rows), jnp.float32),
            pltpu.VMEM((4, 8, 128), jnp.float32),
            pltpu.VMEM((4, top, 8, 128), jnp.float32),
            dma((rows // TILE,)),
            dma,
            dma((CORES, n_2, n_1, n_z)),
            dma((n_z,)),
            dma((n_z, n_1)),
            dma((n_1, n_z, n_2)),
            dma((n_2, n_1, n_z)),
            dma((4, top)),
            dma((4, top)),
        ],
        compiler_params=pltpu.CompilerParams(
            collective_id=0, has_side_effects=True, vmem_limit_bytes=60 * 1024 * 1024
        ),
        name="cover_all",
    )(mine, points, weights[None, :], medoid_ids[None, :])
    return cover.reshape(rows), total[0, 0]


def solution(mesh):
    return jax.shard_map(
        body,
        mesh=mesh,
        in_specs=(P(("pts", "med"), None), P(("pts", "med")), P()),
        out_specs=(P(("pts", "med")), P()),
        check_vma=False,
    )
```

time: 148 us -> 62.7 us (0.42)
  Pallas kernels: 0 us -> 59.3 us
  blocking collectives: 50.9 us -> 0 us
  waiting for transfers between devices: 38.4 us -> 0 us
  matrix products: 23.2 us -> 0 us
  between operations: 16.6 us -> 0.65 us
  other arithmetic: 12.3 us -> 0 us
  local copies, waits for them, and re-layouts: 6.06 us -> 2.48 us
    pallas_call x0 -> x2, Pallas kernels: none -> 59.3 us  [the longest x1 54.9 us: body(): pl.pallas_call(functools.partial(cover_kernel, group_pts, group_med), out...]
    psum x1 -> x0, blocking collectives: 39.2 us -> none  [body(): lax.psum(jnp.stack([jnp.sum(weights * cover), jnp.sum(weights)]), ('pts',...]
    all_gather x1 -> x0, waiting for transfers between devices: 38.3 us -> none  [body(): piece = lax.all_gather(block, 'med', axis=0, tiled=True)]
    dot_general x1 -> x0, matrix products: 23.2 us -> none  [best_match(): lax.dot_general(unit, block, (((1,), (1,)), ((), ())), precision=lax.Prec...]
    all_gather x1 -> x0, blocking collectives: 11.7 us -> none  [body(): block = lax.all_gather(mine, 'pts', axis=0, tiled=True)]
    reduce_sum x5 -> x0, other arithmetic: 5.76 us -> none  [the longest x1 4.15 us: body(): jnp.sum(points * points, axis=1, keepdims=True) + EPS]
    gather x1 -> x0, local copies, waits for them, and re-layouts: 4.02 us -> none  [body(): mine = jnp.take(unit, position, axis=0) * valid[:, None].astype(jnp.float32)]
    mul x2 -> x0, other arithmetic: 3.91 us -> none  [the longest x1 3.83 us: body(): points * lax.rsqrt(jnp.sum(points * points, axis=1, keepdims=True) + EPS)]
  transfers between devices with their start and end apart: 1 -> 0, of which waited for: 1 -> 0; matrix products, arithmetic and copies ran while one was open for 0% -> 0% of each run, Pallas kernels for 0% -> 0%
where the time goes in v1:
time: 62.7 us; the launch traced here: 62.4 us
  Pallas kernels  59.3 us (95%)
  local copies, waits for them, and re-layouts  2.48 us (4%)
  between operations  0.65 us (1%)
    pallas_call x1, Pallas kernels, body(): pl.pallas_call(functools.partial(cover_kernel, group_pts, group_med), out...  54.9 us
    pallas_call x1, Pallas kernels, body(): pl.pallas_call(gather_kernel, out_shape=jax.ShapeDtypeStruct((CAPACITY, w...  4.4 us
    unnamed x1, local copies, waits for them, and re-layouts  1.29 us

profile of v1, /device:TPU:0, one launch (start us, length us, event | category | flops | bytes accessed | tf_op | source)
XLA Modules:
  0.0 62.4 jit_solution(4689709504482038722)
XLA Ops:
  0.6 4.4 %gather_rows.1.mine_ref = f32[24,1024]{1,0:T(8,128)} custom-call(s32[1]{0:T(128)} %bitcast.start_ref, s32[512]{0:T(512)} %ids_ref.1, f32[2048,1024]{1,0:T(8,128)} %points_ref.3), custom_call_target="tpu_custom_call" | custom-call | tf_op jit(solution)/shard_map/gather_rows/pallas_call | solution.py:339
  5.0 54.9 %cover_all.1 = (f32[1,2048]{1,0:T(1,128)}, f32[8,128]{1,0:T(8,128)}) custom-call(f32[24,1024]{1,0:T(8,128)} %gather_rows.1.mine_ref, f32[2048,1024]{1,0:T(8,128)} %points_ref.3, f32[1,2048]{1,0:T(1,128)} %bitcast.6, s32[1,512]{1,0:T(1,128)} %bitcast.7), custom_call_target="tpu_custom_call" | custom-call | tf_op jit(solution)/shard_map/cover_all/pallas_call | solution.py:355
  59.9 1.2 %slice.3 = f32[1,1]{1,0:T(1,128)} slice(f32[8,128]{1,0:T(8,128)} %get-tuple-element.5), slice={[0:1], [0:1]} | slice | bytes 8 | tf_op jit(solution)/shard_map/slice | solution.py:390
  61.1 1.3 %copy.6 = f32[2048]{0:T(1024)} copy(f32[2048]{0:T(1024)} %bitcast.5) | data formatting | bytes 16384

commit v2 on v1

--- a/solution.py
+++ b/solution.py
@@ -12,6 +12,7 @@
 EPS = 1e-06
 CORES = 2
 TILE = 256
+PIECE = 32
 
 
 def gather_kernel(start_ref, ids_ref, points_ref, out_ref, pos_ref, buf_ref, sem):
@@ -50,7 +51,7 @@
 
 def cover_kernel(
     group_pts, group_med, mine_ref, points_ref, weights_ref, ids_ref, cover_ref, total_ref,
-    recv, pbuf, phigh, plow, chigh, clow, offs, best, scale, part, tin,
+    recv, pbuf, pcat, ccat, offs, lanes, best, part, tin,
     psem, msem, rsem, zsem, fsem, ssem, bsem, tsend, trecv,
 ):
     rows = points_ref.shape[0]
@@ -90,12 +91,14 @@
         return {"pts": pts_of(core, i_1, lax.rem(i_2 + step, n_2)), "med": me_med}
 
     sibling = {"pts": me_pts, "med": zed * CORES + other}
-    partners = (
-        [dev_z(step) for step in range(1, n_z)]
-        + [dev_1(step) for step in range(1, n_1)]
-        + [dev_2(step) for step in range(1, n_2)]
-        + [sibling]
-    )
+    plane = group_pts * CORES
+    place = me_pts * CORES + core
+
+    def dev_plane(step):
+        at = lax.rem(place + step, plane)
+        return {"pts": at // CORES, "med": zed * CORES + lax.rem(at, CORES)}
+
+    partners = [dev_z(step) for step in range(1, n_z)] + [dev_plane(step) for step in range(1, plane)]
 
     def points_copy(tile):
         part_of = pl.ds(pl.multiple_of(tile * TILE, TILE), TILE)
@@ -108,6 +111,28 @@
     barrier = pltpu.get_barrier_semaphore()
     for partner in partners:
         pl.semaphore_signal(barrier, inc=1, device_id=partner, device_id_type=pl.DeviceIdType.MESH)
+
+    width = n_z * CAPACITY
+    depth = points_ref.shape[1]
+    ids = ids_ref[...]
+
+    def offsets(which, j_2, j_1):
+        at = lax.broadcasted_iota(jnp.int32, (width, 1), 0)
+        z = at // CAPACITY
+        slot = at - z * CAPACITY
+        first = (pts_of(which, j_1, j_2) * group_med + z * CORES + which) * rows
+        inside = jnp.logical_and(ids >= first, ids < first + rows)
+        count = jnp.sum(jnp.where(inside, 1.0, 0.0), axis=1, keepdims=True)
+        offs[which, j_2, j_1] = jnp.where(slot.astype(jnp.float32) < count, 0.0, -1e30)
+
+    def offsets_at(at, carry):
+        which = at // (n_1 * n_2)
+        j_2 = lax.rem(at, n_1 * n_2) // n_1
+        offsets(which, j_2, lax.rem(at, n_1))
+        return carry
+
+    lax.fori_loop(0, CORES * n_1 * n_2, offsets_at, 0)
+    best[...] = jnp.full(best.shape, -1e30, jnp.float32)
     pl.semaphore_wait(barrier, len(partners))
 
     def send(src, j_2, j_1, z, sem, partner):
@@ -156,21 +181,24 @@
         send_z(step).start()
     send_b(i_2, i_1, zed, mine_ref).start()
 
-    best[...] = jnp.full(best.shape, -1e30, jnp.float32)
-
     def prepare(tile, carry):
         points_copy(tile).wait()
-        part_of = pl.ds(pl.multiple_of(tile * TILE, TILE), TILE)
-        value = pbuf[part_of, :]
-        high, low = split(value)
-        phigh[part_of, :] = high
-        plow[part_of, :] = low
-        square = value * value
-        lanes = square[:, :128]
-        for k in range(1, square.shape[1] // 128):
-            lanes = lanes + square[:, k * 128 : (k + 1) * 128]
-        norm = jnp.sum(lanes.T, axis=0, keepdims=True)
-        scale[:, part_of] = jnp.broadcast_to(lax.rsqrt(norm + EPS), (8, TILE))
+
+        def piece(step, carry):
+            part_of = pl.ds(pl.multiple_of(tile * TILE + step * PIECE, PIECE), PIECE)
+            value = pbuf[part_of, :]
+            high, low = split(value)
+            pcat[part_of, 0:depth] = high
+            pcat[part_of, depth : 2 * depth] = low
+            pcat[part_of, 2 * depth : 3 * depth] = high
+            square = value * value
+            total = square[:, :128]
+            for k in range(1, depth // 128):
+                total = total + square[:, k * 128 : (k + 1) * 128]
+            lanes[part_of, :] = total
+            return carry
+
+        lax.fori_loop(0, TILE // PIECE, piece, 0)
         return carry
 
     lax.fori_loop(0, tiles, prepare, 0)
@@ -186,30 +214,24 @@
             send_2(i_1, z, hop).start()
         send_b(i_2, i_1, z).start()
 
-    width = n_z * CAPACITY
-    ids = ids_ref[...]
-
     def load_chunk(which, j_2, j_1, base):
-        value = recv[which, j_2, j_1].reshape(width, recv.shape[-1])
-        high, low = split(value)
-        chigh[base : base + width, :] = high
-        clow[base : base + width, :] = low
-        at = lax.broadcasted_iota(jnp.int32, (width, 1), 0)
-        z = at // CAPACITY
-        slot = at - z * CAPACITY
-        first = (pts_of(which, j_1, j_2) * group_med + z * CORES + which) * rows
-        inside = jnp.logical_and(ids >= first, ids < first + rows)
-        count = jnp.sum(jnp.where(inside, 1.0, 0.0), axis=1, keepdims=True)
-        offs[base : base + width, :] = jnp.where(slot.astype(jnp.float32) < count, 0.0, -1e30)
+        def pair(step, carry):
+            value = recv[which, j_2, j_1, pl.ds(step * 2, 2)].reshape(2 * CAPACITY, depth)
+            high, low = split(value)
+            part_of = pl.ds(pl.multiple_of(base + step * 2 * CAPACITY, 2 * CAPACITY), 2 * CAPACITY)
+            ccat[part_of, 0:depth] = high
+            ccat[part_of, depth : 2 * depth] = high
+            ccat[part_of, 2 * depth : 3 * depth] = low
+            return carry
+
+        lax.fori_loop(0, n_z // 2, pair, 0)
 
     dims = (((1,), (1,)), ((), ()))
 
-    def multiply(tile):
+    def multiply(tile, mask):
         part_of = pl.ds(pl.multiple_of(tile * TILE, TILE), TILE)
-        dot = functools.partial(lax.dot_general, dimension_numbers=dims, preferred_element_type=jnp.float32)
-        high, low = phigh[part_of, :], plow[part_of, :]
-        sims = dot(clow[...], high) + dot(chigh[...], low) + dot(chigh[...], high)
-        sims = sims + offs[...]
+        sims = lax.dot_general(ccat[...], pcat[part_of, :], dims, preferred_element_type=jnp.float32)
+        sims = sims + mask()
         top = jnp.max(sims.reshape(-1, 8, TILE), axis=0)
         best[:, part_of] = jnp.maximum(best[:, part_of], top)
 
@@ -235,18 +257,21 @@
                 s_2, s_1 = lax.rem(o_2 + e_2, n_2), lax.rem(o_1 + e_1, n_1)
             else:
                 s_2, s_1 = two_at(e_2), one_at(e_1)
-            if not (e_2 == 0 and e_1 == 0):
-                pass
             arrived(other, s_2, s_1, z)
         load_chunk(core, two_at(e_2), one_at(e_1), 0)
         load_chunk(other, s_2, s_1, width)
+
+        def mask():
+            return jnp.concatenate(
+                [offs[core, two_at(e_2), one_at(e_1)], offs[other, s_2, s_1]], axis=0
+            )
 
         def step(tile, carry):
             if events:
                 @pl.when(tile < events)
                 def _():
                     event(tile)
-            multiply(tile)
+            multiply(tile, mask)
             return carry
 
         lax.fori_loop(0, tiles, step, 0)
@@ -256,6 +281,11 @@
                 return carry
 
             lax.fori_loop(tiles, events, rest, 0)
+
+    norms = [
+        jnp.sum(lanes[k * 128 : (k + 1) * 128, :].T, axis=0, keepdims=True) for k in range(rows // 128)
+    ]
+    scale = lax.rsqrt(jnp.concatenate(norms, axis=1) + EPS)
 
     order = [(e_2, e_1) for e_2 in range(n_2) for e_1 in range(n_1)]
     for e_2, e_1 in order:
@@ -275,7 +305,7 @@
         else:
             chunk(e_2, e_1, None, 0)
 
-    cover = jnp.max(best[...], axis=0, keepdims=True) * scale[0:1, :]
+    cover = jnp.max(best[...], axis=0, keepdims=True) * scale
     cover_ref[...] = cover
     weights = weights_ref[...]
     lane = lax.broadcasted_iota(jnp.int32, (8, 128), 1)
@@ -283,9 +313,7 @@
     weight = jnp.sum(weights, axis=1, keepdims=True)
     value = jnp.where(lane == 0, number, weight)
 
-    stages = [
-        (n_z, zed, dev_z), (n_1, i_1, dev_1), (n_2, i_2, dev_2), (CORES, core, lambda step: sibling),
-    ]
+    stages = [(n_z, zed, dev_z), (plane, place, dev_plane)]
     copies = []
     for stage, (extent, index, partner_of) in enumerate(stages):
         if extent == 1:
@@ -326,6 +354,11 @@
         copy.wait_send()
 
 
+def finish_kernel(cover_ref, total_ref, out_ref, mean_ref):
+    out_ref[...] = cover_ref[...]
+    mean_ref[0, 0] = total_ref[0, 0]
+
+
 def body(points, weights, medoid_ids):
     rows, width = points.shape
     group_pts = lax.axis_size("pts")
@@ -350,7 +383,7 @@
     )(start[None].astype(jnp.int32), medoid_ids, points)
 
     chunk = CORES * n_z * CAPACITY
-    top = max(n_z, n_1, n_2, CORES)
+    top = max(n_z, group_pts * CORES)
     dma = pltpu.SemaphoreType.DMA
     cover, total = pl.pallas_call(
         functools.partial(cover_kernel, group_pts, group_med),
@@ -363,15 +396,13 @@
         scratch_shapes=[
             pltpu.VMEM((CORES, n_2, n_1, n_z, CAPACITY, width), jnp.float32),
             pltpu.VMEM((rows, width), jnp.float32),
-            pltpu.VMEM((rows, width), jnp.bfloat16),
-            pltpu.VMEM((rows, width), jnp.bfloat16),
-            pltpu.VMEM((chunk, width), jnp.bfloat16),
-            pltpu.VMEM((chunk, width), jnp.bfloat16),
-            pltpu.VMEM((chunk, 1), jnp.float32),
+            pltpu.VMEM((rows, 3 * width), jnp.bfloat16),
+            pltpu.VMEM((chunk, 3 * width), jnp.bfloat16),
+            pltpu.VMEM((CORES, n_2, n_1, n_z * CAPACITY, 1), jnp.float32),
+            pltpu.VMEM((rows, 128), jnp.float32),
             pltpu.VMEM((8, rows), jnp.float32),
-            pltpu.VMEM((8, rows), jnp.float32),
-            pltpu.VMEM((4, 8, 128), jnp.float32),
-            pltpu.VMEM((4, top, 8, 128), jnp.float32),
+            pltpu.VMEM((2, 8, 128), jnp.float32),
+            pltpu.VMEM((2, top, 8, 128), jnp.float32),
             dma((rows // TILE,)),
             dma,
             dma((CORES, n_2, n_1, n_z)),
@@ -379,15 +410,25 @@
             dma((n_z, n_1)),
             dma((n_1, n_z, n_2)),
             dma((n_2, n_1, n_z)),
-            dma((4, top)),
-            dma((4, top)),
+            dma((2, top)),
+            dma((2, top)),
         ],
         compiler_params=pltpu.CompilerParams(
             collective_id=0, has_side_effects=True, vmem_limit_bytes=60 * 1024 * 1024
         ),
         name="cover_all",
     )(mine, points, weights[None, :], medoid_ids[None, :])
-    return cover.reshape(rows), total[0, 0]
+    cover, total = pl.pallas_call(
+        finish_kernel,
+        out_shape=[
+            jax.ShapeDtypeStruct((1, rows), jnp.float32),
+            jax.ShapeDtypeStruct((1, 1), jnp.float32),
+        ],
+        in_specs=[vmem, vmem],
+        out_specs=[vmem, smem],
+        name="finish",
+    )(cover, total)
+    return cover.reshape(rows), total.reshape(())
 
 
 def solution(mesh):

time: 62.7 us -> 58.4 us (0.931)
  local copies, waits for them, and re-layouts: 2.48 us -> 0 us
  Pallas kernels: 59.3 us -> 57.5 us
    pallas_call x1, Pallas kernels: 54.9 us -> 51.7 us  [body(): pl.pallas_call(functools.partial(cover_kernel, group_pts, group_med), out...]
    pallas_call x0 -> x1, Pallas kernels: none -> 1.31 us  [body(): pl.pallas_call(finish_kernel, out_shape=[jax.ShapeDtypeStruct((1, rows),...]
    unnamed x1 -> x0, local copies, waits for them, and re-layouts: 1.29 us -> none
    slice x1 -> x0, local copies, waits for them, and re-layouts: 1.18 us -> none  [body(): return (cover.reshape(rows), total[0, 0])]
where the time goes in v2:
time: 58.4 us; the launch traced here: 58.1 us
  Pallas kernels  57.5 us (98%)
  between operations  0.65 us (1%)
    pallas_call x1, Pallas kernels, body(): pl.pallas_call(functools.partial(cover_kernel, group_pts, group_med), out...  51.7 us
    pallas_call x1, Pallas kernels, body(): pl.pallas_call(gather_kernel, out_shape=jax.ShapeDtypeStruct((CAPACITY, w...  4.42 us
    pallas_call x1, Pallas kernels, body(): pl.pallas_call(finish_kernel, out_shape=[jax.ShapeDtypeStruct((1, rows),...  1.31 us

profile of v2, /device:TPU:0, one launch (start us, length us, event | category | flops | bytes accessed | tf_op | source)
XLA Modules:
  0.0 58.1 jit_solution(12685593046224752597)
XLA Ops:
  0.6 4.4 %gather_rows.1.mine_ref = f32[24,1024]{1,0:T(8,128)} custom-call(s32[1]{0:T(128)} %bitcast.start_ref, s32[512]{0:T(512)} %ids_ref.1, f32[2048,1024]{1,0:T(8,128)} %points_ref.3), custom_call_target="tpu_custom_call" | custom-call | tf_op jit(solution)/shard_map/gather_rows/pallas_call | solution.py:372
  5.1 51.7 %cover_all.1 = (f32[1,2048]{1,0:T(1,128)}, f32[8,128]{1,0:T(8,128)}) custom-call(f32[24,1024]{1,0:T(8,128)} %gather_rows.1.mine_ref, f32[2048,1024]{1,0:T(8,128)} %points_ref.3, f32[1,2048]{1,0:T(1,128)} %bitcast.5, s32[1,512]{1,0:T(1,128)} %bitcast.6), custom_call_target="tpu_custom_call" | custom-call | tf_op jit(solution)/shard_map/cover_all/pallas_call | solution.py:388
  56.8 1.3 %finish.1 = (f32[1,2048]{1,0:T(1,128)}, f32[1,1]{1,0:T(1,128)}) custom-call(f32[1,2048]{1,0:T(1,128)} %get-tuple-element.6.cover_ref, f32[8,128]{1,0:T(8,128)} %get-tuple-element.7.total_ref), custom_call_target="tpu_custom_call" | custom-call | tf_op jit(solution)/shard_map/finish/pallas_call | solution.py:421

commit v3 on v2

--- a/solution.py
+++ b/solution.py
@@ -12,7 +12,7 @@
 EPS = 1e-06
 CORES = 2
 TILE = 256
-PIECE = 32
+PIECE = 128
 
 
 def gather_kernel(start_ref, ids_ref, points_ref, out_ref, pos_ref, buf_ref, sem):
@@ -51,7 +51,7 @@
 
 def cover_kernel(
     group_pts, group_med, mine_ref, points_ref, weights_ref, ids_ref, cover_ref, total_ref,
-    recv, pbuf, pcat, ccat, offs, lanes, best, part, tin,
+    recv, pbuf, pcat, ccat, offs, scale_ref, best, part, tin,
     psem, msem, rsem, zsem, fsem, ssem, bsem, tsend, trecv,
 ):
     rows = points_ref.shape[0]
@@ -186,16 +186,16 @@
 
         def piece(step, carry):
             part_of = pl.ds(pl.multiple_of(tile * TILE + step * PIECE, PIECE), PIECE)
-            value = pbuf[part_of, :]
-            high, low = split(value)
-            pcat[part_of, 0:depth] = high
-            pcat[part_of, depth : 2 * depth] = low
-            pcat[part_of, 2 * depth : 3 * depth] = high
-            square = value * value
-            total = square[:, :128]
-            for k in range(1, depth // 128):
-                total = total + square[:, k * 128 : (k + 1) * 128]
-            lanes[part_of, :] = total
+            total = jnp.zeros((8, PIECE), jnp.float32)
+            for k in range(0, depth, 128):
+                value = pbuf[part_of, k : k + 128].T
+                high, low = split(value)
+                pcat[k : k + 128, part_of] = high
+                pcat[depth + k : depth + k + 128, part_of] = low
+                pcat[2 * depth + k : 2 * depth + k + 128, part_of] = high
+                total = total + jnp.sum((value * value).reshape(-1, 8, PIECE), axis=0)
+            norm = jnp.sum(total, axis=0, keepdims=True)
+            scale_ref[:, part_of] = lax.rsqrt(norm + EPS)
             return carry
 
         lax.fori_loop(0, TILE // PIECE, piece, 0)
@@ -226,11 +226,11 @@
 
         lax.fori_loop(0, n_z // 2, pair, 0)
 
-    dims = (((1,), (1,)), ((), ()))
+    dims = (((1,), (0,)), ((), ()))
 
     def multiply(tile, mask):
         part_of = pl.ds(pl.multiple_of(tile * TILE, TILE), TILE)
-        sims = lax.dot_general(ccat[...], pcat[part_of, :], dims, preferred_element_type=jnp.float32)
+        sims = lax.dot_general(ccat[...], pcat[:, part_of], dims, preferred_element_type=jnp.float32)
         sims = sims + mask()
         top = jnp.max(sims.reshape(-1, 8, TILE), axis=0)
         best[:, part_of] = jnp.maximum(best[:, part_of], top)
@@ -281,11 +281,6 @@
                 return carry
 
             lax.fori_loop(tiles, events, rest, 0)
-
-    norms = [
-        jnp.sum(lanes[k * 128 : (k + 1) * 128, :].T, axis=0, keepdims=True) for k in range(rows // 128)
-    ]
-    scale = lax.rsqrt(jnp.concatenate(norms, axis=1) + EPS)
 
     order = [(e_2, e_1) for e_2 in range(n_2) for e_1 in range(n_1)]
     for e_2, e_1 in order:
@@ -305,7 +300,7 @@
         else:
             chunk(e_2, e_1, None, 0)
 
-    cover = jnp.max(best[...], axis=0, keepdims=True) * scale
+    cover = jnp.max(best[...], axis=0, keepdims=True) * scale_ref[...]
     cover_ref[...] = cover
     weights = weights_ref[...]
     lane = lax.broadcasted_iota(jnp.int32, (8, 128), 1)
@@ -396,10 +391,10 @@
         scratch_shapes=[
             pltpu.VMEM((CORES, n_2, n_1, n_z, CAPACITY, width), jnp.float32),
             pltpu.VMEM((rows, width), jnp.float32),
-            pltpu.VMEM((rows, 3 * width), jnp.bfloat16),
+            pltpu.VMEM((3 * width, rows), jnp.bfloat16),
             pltpu.VMEM((chunk, 3 * width), jnp.bfloat16),
             pltpu.VMEM((CORES, n_2, n_1, n_z * CAPACITY, 1), jnp.float32),
-            pltpu.VMEM((rows, 128), jnp.float32),
+            pltpu.VMEM((1, rows), jnp.float32),
             pltpu.VMEM((8, rows), jnp.float32),
             pltpu.VMEM((2, 8, 128), jnp.float32),
             pltpu.VMEM((2, top, 8, 128), jnp.float32),

time: 58.4 us -> 53.7 us (0.920)
  Pallas kernels: 57.5 us -> 52.8 us
    pallas_call x1, Pallas kernels: 51.7 us -> 47 us  [body(): pl.pallas_call(functools.partial(cover_kernel, group_pts, group_med), out...]
where the time goes in v3:
time: 53.7 us; the launch traced here: 53.4 us
  Pallas kernels  52.8 us (98%)
  between operations  0.65 us (1%)
    pallas_call x1, Pallas kernels, body(): pl.pallas_call(functools.partial(cover_kernel, group_pts, group_med), out...  47 us
    pallas_call x1, Pallas kernels, body(): pl.pallas_call(gather_kernel, out_shape=jax.ShapeDtypeStruct((CAPACITY, w...  4.52 us
    pallas_call x1, Pallas kernels, body(): pl.pallas_call(finish_kernel, out_shape=[jax.ShapeDtypeStruct((1, rows),...  1.31 us

profile of v3, /device:TPU:0, one launch (start us, length us, event | category | flops | bytes accessed | tf_op | source)
XLA Modules:
  0.0 53.4 jit_solution(7137001329989785856)
XLA Ops:
  0.6 4.5 %gather_rows.1.mine_ref = f32[24,1024]{1,0:T(8,128)} custom-call(s32[1]{0:T(128)} %bitcast.start_ref, s32[512]{0:T(512)} %ids_ref.1, f32[2048,1024]{1,0:T(8,128)} %points_ref.3), custom_call_target="tpu_custom_call" | custom-call | tf_op jit(solution)/shard_map/gather_rows/pallas_call | solution.py:367
  5.2 47.0 %cover_all.1 = (f32[1,2048]{1,0:T(1,128)}, f32[8,128]{1,0:T(8,128)}) custom-call(f32[24,1024]{1,0:T(8,128)} %gather_rows.1.mine_ref, f32[2048,1024]{1,0:T(8,128)} %points_ref.3, f32[1,2048]{1,0:T(1,128)} %bitcast.5, s32[1,512]{1,0:T(1,128)} %bitcast.6), custom_call_target="tpu_custom_call" | custom-call | tf_op jit(solution)/shard_map/cover_all/pallas_call | solution.py:383
  52.1 1.3 %finish.1 = (f32[1,2048]{1,0:T(1,128)}, f32[1,1]{1,0:T(1,128)}) custom-call(f32[1,2048]{1,0:T(1,128)} %get-tuple-element.6.cover_ref, f32[8,128]{1,0:T(8,128)} %get-tuple-element.7.total_ref), custom_call_target="tpu_custom_call" | custom-call | tf_op jit(solution)/shard_map/finish/pallas_call | solution.py:416
